TPU v7x, 32 devices: a whole 2x2x4 slice. The times are simulated.
32 devices in a mesh: row: 4 (over z), col: 8 (over y, x, core).
Axes of the slice: x: 2, y: 2, z: 4, core: 2. Of those that a mesh axis runs over, the one named last changes fastest.
Arguments:
- working: float32 [16, 4, 256, 8, 8, 256], P(None, 'row', None, None, 'col'), may hold values from -6 to 6
- factor_panel: float32 [2, 16, 4, 256, 256], P(None, None, 'row'), may hold values from -0.12 to 2, as said below
Outputs:
- gram_part: float32 [16, 4, 256, 8, 8, 256], P(None, 'row', None, None, 'col')
- finished_columns: float32 [8, 4, 256, 8, 4, 512], P(None, None, None, 'col', 'row')
Inputs may be any that keep to these rules, and one draw needn't show every extreme that they name: factor_panel holds a lower-triangular factor: entries above the factor's diagonal are zero and its diagonal entries lie between 1 and 2.
All inputs are finite; a program needn't handle non-finite values.
Results may differ from a plain program's by a relative error of at most 0.0001.
Values sent between devices are 32-bit elements; how exact they have to be, the bound alone decides.
No kernel may reach another device: no remote copies, remote signals or barrier semaphores. Data moves between devices by JAX's collectives and lax.ppermute only.
A program may use at most 256 MiB of HBM per device.

v0:
```python
import jax
import jax.numpy as jnp
from jax import lax
from jax.sharding import PartitionSpec as P

BLK = 256
K = 30
STEPS = 2


def from_root(value, axis, source):
    kept = jnp.where(lax.axis_index(axis) == source, value, 0).astype(value.dtype)
    return lax.psum(kept, axis)


def per_device(working, factor_panel):
    row_count = lax.axis_size("row")
    col_count = lax.axis_size("col")
    row_index = lax.axis_index("row")
    blocks_rows = working.shape[0]
    width = working.shape[2]
    blocks_cols = working.shape[3]
    matrix_rows = working.reshape(blocks_rows, width, blocks_cols * width)
    global_block = jnp.arange(blocks_rows) * row_count + row_index
    solved_list = []
    for step_index in range(STEPS):
        target = K + step_index
        slab = matrix_rows[target // row_count]
        solve_target = K + step_index
        owner = solve_target % row_count
        diagonal = jnp.tril(factor_panel[step_index, solve_target // row_count, 0])
        diagonal = jnp.where(row_index == owner, diagonal, jnp.eye(width, dtype=jnp.float32))
        solve_solved = lax.linalg.triangular_solve(diagonal, slab, left_side=True, lower=True)
        solved = from_root(solve_solved, "row", owner)
        column_part = factor_panel[step_index, :, 0]
        eliminate_target = K + step_index
        updated = matrix_rows - jnp.einsum(
            "rab,bc->rac", column_part, solved, precision=lax.Precision.HIGHEST
        )
        below = (global_block > eliminate_target)[:, None, None]
        here = (global_block == eliminate_target)[:, None, None]
        matrix_rows = jnp.where(below, updated, jnp.where(here, solved[None], matrix_rows))
        solved_list.append(solved)
    stacked = jnp.concatenate(solved_list, 0)
    depth = stacked.shape[0]
    owners_count = col_count // row_count
    pieces = [
        from_root(stacked.reshape(depth, blocks_cols, width), "col", row_index + offset * row_count)
        for offset in range(owners_count)
    ]
    chosen = jnp.stack(pieces, 2)
    row_panels = chosen.reshape(depth, blocks_rows * width)
    gram = lax.dot_general(
        row_panels, stacked, (((0,), (0,)), ((), ())), precision=lax.Precision.HIGHEST
    )
    gram = (gram * (1.0 / (STEPS * BLK))).reshape(blocks_rows, 1, width, blocks_cols, 1, width)
    finished_count = (K + STEPS) // row_count
    finished = matrix_rows[:finished_count].reshape(finished_count, 1, width, 1, row_count, -1)
    moved = lax.all_to_all(finished, "row", split_axis=4, concat_axis=1, tiled=True)
    return (gram, moved)


def solution(mesh):
    placed = (P(None, "row", None, None, "col", None), P(None, None, "row", None, None))
    return jax.shard_map(
        per_device,
        mesh=mesh,
        in_specs=placed,
        out_specs=(
            P(None, "row", None, None, "col", None),
            P(None, None, None, "col", "row", None),
        ),
        check_vma=False,
    )
```

profile of v0, /device:TPU:0, one launch (start us, length us, event | category | flops | bytes accessed | tf_op | source)
XLA Modules:
  0.0 810.8 jit_solution(15085424552516502196)
XLA Ops:
  7.2 1.1 fusion.9
  8.3 0.1 broadcast.96
  8.4 4.0 while.4
  8.4 0.6 fusion.24
  9.0 1.4 bitcast_dynamic-update-slice_fusion.4
  10.4 0.6 fusion.24
  11.0 1.4 bitcast_dynamic-update-slice_fusion.4
  12.4 19.7 %custom-call.4 = f32[2,128,128]{1,2,0:T(8,128)S(1)} custom-call(f32[2,128,128]{2,1,0:T(8,128)S(1)} %get-tuple-element.17), custom_call_target="InvertDiagBlocksLowerTriangular" | custom-call | tf_op jit(solution)/shard_map/triangular_solve/custom-call.1 | solution.py:33
  32.1 7.2 slice_reduce_fusion
  39.2 0.9 copy.44
  40.1 1.1 fusion.6
  41.2 1.0 convolution_subtract_fusion.1
  42.2 1.1 fusion.13
  43.3 1.5 maximum_select_fusion
  44.8 0.0 all-reduce.7.cloned.1.call-start
  44.8 79.1 %copy.24 = f32[16,1,256,8,1,256]{2,5,3,0,4,1:T(8,128)} copy(f32[16,1,256,8,1,256]{5,4,3,2,1,0:T(1,128)} %param.4) | data formatting | bytes 67108864 | tf_op args[0]
  123.9 3.8 while.5
  123.9 0.6 fusion.25
  124.5 1.3 bitcast_dynamic-update-slice_fusion.5
  125.8 0.6 fusion.25
  126.4 1.3 bitcast_dynamic-update-slice_fusion.5
  127.7 19.7 %custom-call.5 = f32[2,128,128]{1,2,0:T(8,128)S(1)} custom-call(f32[2,128,128]{2,1,0:T(8,128)S(1)} %get-tuple-element.18), custom_call_target="InvertDiagBlocksLowerTriangular" | custom-call | tf_op jit(solution)/shard_map/triangular_solve/custom-call.1 | solution.py:33
  147.4 1.9 copy.27
  149.3 73.5 %fusion = f32[16,256,2048]{1,2,0:T(8,128)} fusion(f32[16,256,2048]{1,2,0:T(8,128)} %bitcast.82, f32[256,2048]{0,1:T(8,128)S(1)} %copy.27, pred[16]{0:T(512)(128)(4,1)S(1)} %get-tuple-element.53, pred[16]{0:T(512)(128)(4,1)S(1)} %get-tuple-element.54, f32[2,16,1,256,256]{4,3,1,2,0:T(8,128)} %bitcast.86, f32[256,2048]{1,0:T(8,128)} %all-reduce.5.cloned.1.call-done), kind=kOutput, calls=%fused_computation.5 | convolution fusion | flops 25794969600 | bytes 75497504 | tf_op jit(solution)/shard_map/rab,bc->rac/dot_general | solution.py:37
  222.9 1.7 slice_bitcast_fusion.4
  224.6 1.1 fusion.4
  225.7 1.8 convolution_subtract_fusion
  227.5 1.1 fusion.11
  228.6 1.5 maximum_select_fusion.1
  230.1 89.0 %all-reduce.7.cloned.1.call-done = f32[256,2048]{1,0:T(8,128)} async-done(((f32[256,2048]{1,0:T(8,128)}), f32[256,2048]{1,0:T(8,128)}) %all-reduce.7.cloned.1.call-update) | async-done | bytes 2097168 | tf_op jit(solution)/shard_map/psum | solution.py:13
  319.1 58.3 %convolution_bitcast_fusion = f32[16,256,2048]{1,2,0:T(8,128)} fusion(f32[2,16,1,256,256]{4,3,1,2,0:T(8,128)} %bitcast.87, f32[256,2048]{1,0:T(8,128)} %all-reduce.7.cloned.1.call-done), kind=kOutput, calls=%fused_computation.6 | convolution fusion | flops 25769803776 | bytes 39845888 | tf_op jit(solution)/shard_map/rab,bc->rac/dot_general | solution.py:37
  377.4 1.8 copy.33
  379.2 18.5 %fusion.1 = f32[8,256,2048]{1,2,0:T(8,128)} fusion(f32[16,256,2048]{1,2,0:T(8,128)} %convolution_bitcast_fusion, f32[16,256,2048]{1,2,0:T(8,128)} %fusion, f32[256,2048]{0,1:T(8,128)} %copy.33, pred[8]{0:T(512)(128)(4,1)S(1)} %bitcast.93, pred[8]{0:T(512)(128)(4,1)S(1)} %bitcast.92), kind=kLoop, calls=%fused_computation.9 | loop fusion | flops 12582912 | bytes 52428816 | tf_op jit(solution)/shard_map/jit(_where)/select_n | solution.py:42
  397.8 16.4 %copy.34 = f32[8,1,256,1,4,512]{5,2,0,3,1,4:T(8,128)} copy(f32[8,1,256,1,4,512]{2,5,4,0,3,1:T(8,128)} %bitcast.83) | data formatting | bytes 33554432 | tf_op jit(solution)/shard_map/reshape | solution.py:58
  414.1 7.2 all-to-all-start
  421.3 0.0 all-reduce.9.cloned.1.call-start
  421.4 0.1 constant_dynamic-update-slice_fusion.1
  421.6 1.4 copy-done.2
  423.0 0.1 constant_dynamic-update-slice_fusion
  423.1 4.6 broadcast_select_fusion.1
  427.8 5.4 copy.41
  433.2 5.3 copy.42
  438.5 127.6 %all-reduce.9.cloned.1.call-done = (f32[512,8,1,256]{0,3,2,1:T(8,128)}, f32[512,8,1,256]{0,3,2,1:T(8,128)}) async-done(((f32[512,8,1,256]{0,3,2,1:T(8,128)}, f32[512,8,1,256]{0,3,2,1:T(8,128)}), (f32[512,8,1,256]{0,3,2,1:T(8,128)}, f32[512,8,1,256]{0,3,2,1:T(8,128)})) %all-reduce.9.cloned.1.call-update) | async-done | bytes 8388624 | tf_op jit(solution)/shard_map/psum | solution.py:13
  566.2 4.7 pad_maximum_fusion
  570.8 58.3 %convolution_multiply_fusion = f32[4096,2048]{1,0:T(8,128)} fusion(f32[512,4096]{0,1:T(8,128)S(1)} %bitcast.90, f32[512,2048]{1,0:T(8,128)S(1)} %copy-done.4), kind=kOutput, calls=%fused_computation.7 | convolution fusion | flops 51547996160 | bytes 46137344 | tf_op jit(solution)/shard_map/dot_general | solution.py:53
  629.2 48.3 %reshape.85 = f32[16,1,256,8,1,256]{5,4,3,2,1,0:T(1,128)} reshape(f32[4096,2048]{1,0:T(8,128)} %convolution_multiply_fusion) | data formatting | bytes 67108864 | tf_op jit(solution)/shard_map/reshape | solution.py:56
  677.5 106.6 %all-to-all-done = f32[8,1,256,1,4,512]{5,2,0,3,1,4:T(8,128)} async-done(((f32[8,1,256,1,4,512]{5,2,0,3,1,4:T(8,128)}), f32[8,1,256,1,4,512]{5,2,0,3,1,4:T(8,128)}, u32[]{:S(2)}, u32[]{:S(2)}) %all-to-all-start) | async-done | bytes 16777248 | tf_op jit(solution)/shard_map/all_to_all | solution.py:59
  784.1 19.9 %copy.36 = f32[8,4,256,1,1,512]{5,4,3,2,1,0:T(1,128)} copy(f32[8,4,256,1,1,512]{5,2,0,1,4,3:T(8,128)} %bitcast.22) | data formatting | bytes 33554432
  (23 shorter events, 0.2 us)
Async XLA Ops:
  7.2 140.2 %all-reduce.5.cloned.1.call-start = ((), (), s32[]{:S(2)}) async-start(), calls=%async_computation.1 | async-start | bytes 4194304 | tf_op jit(solution)/shard_map/psum | solution.py:13
  44.8 274.3 %all-reduce.7.cloned.1.call-start = ((), (), s32[]{:S(2)}) async-start(), calls=%async_computation.2 | async-start | bytes 4194304 | tf_op jit(solution)/shard_map/psum | solution.py:13
  319.1 58.3 %copy-start.1 = (f32[256,2048]{1,0:T(8,128)S(1)}, f32[256,2048]{1,0:T(8,128)}, u32[]{:S(2)}) copy-start(f32[256,2048]{1,0:T(8,128)} %all-reduce.7.cloned.1.call-done) | copy-start | bytes 6291460
  414.1 7.3 copy-start
  414.1 370.0 %all-to-all-start = ((f32[8,1,256,1,4,512]{5,2,0,3,1,4:T(8,128)}), f32[8,1,256,1,4,512]{5,2,0,3,1,4:T(8,128)}, u32[]{:S(2)}, u32[]{:S(2)}) async-start(f32[8,1,256,1,4,512]{5,2,0,3,1,4:T(8,128)} %copy.34), calls=%async_computation | async-start | bytes 33554432 | tf_op jit(solution)/shard_map/all_to_all | solution.py:59
  421.3 144.8 %all-reduce.9.cloned.1.call-start = ((), (), s32[]{:S(2)}) async-start(), calls=%async_computation.3 | async-start | bytes 16777216 | tf_op jit(solution)/shard_map/psum | solution.py:13
  421.4 1.6 copy-start.2
  423.1 4.7 copy-start.3
  566.2 4.7 copy-start.4
Sparse Core Ops, SparseCore 0:
  44.9 88.8 all-reduce.4
  230.2 88.8 all-reduce.6
  438.6 127.4 all-reduce.8
where the time goes:
time: 823 us; the launch traced here: 811 us
  waiting for transfers between devices  323 us (39%)
  local copies, waits for them, and re-layouts  197 us (24%)
  matrix products  197 us (24%)
  other arithmetic  71.2 us (9%)
  between operations  14.2 us (2%)
    psum x3, waiting for transfers between devices, from_root(): return lax.psum(kept, axis)  217 us
    dot_general x2, matrix products, per_device(): jnp.einsum('rab,bc->rac', column_part, solved, precision=lax.Precision.HI...  132 us
    all_to_all x1, waiting for transfers between devices, per_device(): lax.all_to_all(finished, 'row', split_axis=4, concat_axis=1, tiled=True)  107 us
    unnamed x14, local copies, waits for them, and re-layouts  101 us
    dot_general x1, matrix products, per_device(): lax.dot_general(row_panels, stacked, (((0,), (0,)), ((), ())), precision=...  58.3 us
    reshape x1, local copies, waits for them, and re-layouts, per_device(): (gram * (1.0 / (STEPS * BLK))).reshape(blocks_rows, 1, width, blocks_cols...  48.3 us
    another operation x4, other arithmetic, per_device(): lax.linalg.triangular_solve(diagonal, slab, left_side=True, lower=True)  40.4 us
    select_n x1, other arithmetic, per_device(): jnp.where(below, updated, jnp.where(here, solved[None], matrix_rows))  18.5 us
  transfers between devices with their start and end apart: 4, of which 3 were waited for; matrix products, arithmetic and copies ran while one was open for 28% of the time, Pallas kernels for 0%

commit v1 on v0

--- a/solution.py
+++ b/solution.py
@@ -10,7 +10,7 @@
 
 def from_root(value, axis, source):
     kept = jnp.where(lax.axis_index(axis) == source, value, 0).astype(value.dtype)
-    return lax.psum(kept, axis)
+    return jnp.sum(lax.all_gather(kept, axis), axis=0)
 
 
 def per_device(working, factor_panel):

time: 823 us -> 1120 us (1.36)
  blocking collectives: 0 us -> 368 us
  waiting for transfers between devices: 323 us -> 184 us
  other arithmetic: 71.2 us -> 114 us
  local copies, waits for them, and re-layouts: 197 us -> 222 us
    all_to_all x0 -> x1, blocking collectives: none -> 368 us  [per_device(): lax.all_to_all(finished, 'row', split_axis=4, concat_axis=1, tiled=True)]
    psum x3 -> x0, waiting for transfers between devices: 217 us -> none  [from_root(): return lax.psum(kept, axis)]
    all_gather x0 -> x4, waiting for transfers between devices: none -> 184 us  [from_root(): return jnp.sum(lax.all_gather(kept, axis), axis=0)]
    all_to_all x1 -> x0, waiting for transfers between devices: 107 us -> none  [per_device(): lax.all_to_all(finished, 'row', split_axis=4, concat_axis=1, tiled=True)]
    reduce_sum x0 -> x4, other arithmetic: none -> 40.3 us  [from_root(): return jnp.sum(lax.all_gather(kept, axis), axis=0)]
    unnamed x14 -> x9, local copies, waits for them, and re-layouts: 101 us -> 124 us
  transfers between devices with their start and end apart: 4 -> 4, of which waited for: 3 -> 2; matrix products, arithmetic and copies ran while one was open for 28% -> 23% of each run, Pallas kernels for 0% -> 0%
where the time goes in v1:
time: 1120 us; the launch traced here: 1100 us
  blocking collectives  368 us (33%)
  local copies, waits for them, and re-layouts  222 us (20%)
  matrix products  200 us (18%)
  waiting for transfers between devices  184 us (16%)
  other arithmetic  114 us (10%)
  between operations  14.3 us (1%)
    all_to_all x1, blocking collectives, per_device(): lax.all_to_all(finished, 'row', split_axis=4, concat_axis=1, tiled=True)  368 us
    all_gather x4, waiting for transfers between devices, from_root(): return jnp.sum(lax.all_gather(kept, axis), axis=0)  184 us
    dot_general x2, matrix products, per_device(): jnp.einsum('rab,bc->rac', column_part, solved, precision=lax.Precision.HI...  134 us
    unnamed x9, local copies, waits for them, and re-layouts  124 us
    dot_general x1, matrix products, per_device(): lax.dot_general(row_panels, stacked, (((0,), (0,)), ((), ())), precision=...  59.2 us
    reshape x1, local copies, waits for them, and re-layouts, per_device(): (gram * (1.0 / (STEPS * BLK))).reshape(blocks_rows, 1, width, blocks_cols...  48.3 us
    another operation x4, other arithmetic, per_device(): lax.linalg.triangular_solve(diagonal, slab, left_side=True, lower=True)  40.4 us
    reduce_sum x4, other arithmetic, from_root(): return jnp.sum(lax.all_gather(kept, axis), axis=0)  40.3 us
  transfers between devices with their start and end apart: 4, of which 2 were waited for; matrix products, arithmetic and copies ran while one was open for 23% of the time, Pallas kernels for 0%

profile of v1, /device:TPU:0, one launch (start us, length us, event | category | flops | bytes accessed | tf_op | source)
XLA Modules:
  0.0 1102.3 jit_solution(8894254093817624835)
XLA Ops:
  7.2 1.1 fusion.11
  8.3 0.1 broadcast.124
  8.4 3.8 while.4
  8.4 0.6 fusion.27
  9.0 1.3 bitcast_dynamic-update-slice_fusion.4
  10.3 0.6 fusion.27
  10.9 1.3 bitcast_dynamic-update-slice_fusion.4
  12.2 19.7 %custom-call.4 = f32[2,128,128]{1,2,0:T(8,128)S(1)} custom-call(f32[2,128,128]{2,1,0:T(8,128)S(1)} %get-tuple-element.17), custom_call_target="InvertDiagBlocksLowerTriangular" | custom-call | tf_op jit(solution)/shard_map/triangular_solve/custom-call.1 | solution.py:33
  31.9 7.2 slice_reduce_fusion
  39.1 0.9 copy.42
  40.0 1.1 fusion.8
  41.0 1.0 convolution_subtract_fusion.1
  42.1 1.1 fusion.15
  43.1 1.5 maximum_select_fusion
  44.7 92.7 %copy.25 = f32[16,1,256,8,1,256]{2,5,3,0,4,1:T(8,128)} copy(f32[16,1,256,8,1,256]{5,4,3,2,1,0:T(1,128)} %param.4) | data formatting | bytes 67108864 | tf_op args[0]
  137.4 4.1 while.5
  137.4 0.6 fusion.28
  138.0 1.4 bitcast_dynamic-update-slice_fusion.5
  139.5 0.6 fusion.28
  140.1 1.4 bitcast_dynamic-update-slice_fusion.5
  141.5 19.7 %custom-call.5 = f32[2,128,128]{1,2,0:T(8,128)S(1)} custom-call(f32[2,128,128]{2,1,0:T(8,128)S(1)} %get-tuple-element.18), custom_call_target="InvertDiagBlocksLowerTriangular" | custom-call | tf_op jit(solution)/shard_map/triangular_solve/custom-call.1 | solution.py:33
  161.2 35.9 %all-gather.11.cloned.1.call-done = f32[1024,2048]{1,0:T(8,128)} async-done(((f32[256,2048]{1,0:T(8,128)}), f32[1024,2048]{1,0:T(8,128)}) %all-gather.11.cloned.1.call-update) | async-done | bytes 8388624 | tf_op jit(solution)/shard_map/all_gather | solution.py:13
  197.1 5.7 reduce_sum.36
  202.8 1.9 copy.28
  204.8 73.3 %fusion = f32[16,256,2048]{1,2,0:T(8,128)} fusion(f32[16,256,2048]{1,2,0:T(8,128)} %bitcast.90, f32[256,2048]{0,1:T(8,128)S(1)} %copy.28, pred[16]{0:T(512)(128)(4,1)S(1)} %get-tuple-element.53, pred[16]{0:T(512)(128)(4,1)S(1)} %get-tuple-element.54, f32[2,16,1,256,256]{4,3,1,2,0:T(8,128)} %bitcast.99, f32[256,2048]{1,0:T(8,128)} %reduce_sum.36), kind=kOutput, calls=%fused_computation.5 | convolution fusion | flops 25794969600 | bytes 75497504 | tf_op jit(solution)/shard_map/rab,bc->rac/dot_general | solution.py:37
  278.1 1.7 slice_bitcast_fusion.4
  279.8 1.1 fusion.6
  280.9 1.8 convolution_subtract_fusion
  282.8 1.1 fusion.13
  283.8 1.5 maximum_select_fusion.1
  285.4 147.9 %all-gather.13.cloned.1.call-done = f32[1024,2048]{1,0:T(8,128)} async-done(((f32[256,2048]{1,0:T(8,128)}), f32[1024,2048]{1,0:T(8,128)}) %all-gather.13.cloned.1.call-update) | async-done | bytes 8388624 | tf_op jit(solution)/shard_map/all_gather | solution.py:13
  433.3 5.9 reduce_sum.37
  439.2 4.9 fusion.3
  444.1 4.0 copy.43
  448.2 0.0 all-gather.9.cloned.1.call-start
  448.2 6.7 copy.44
  454.9 3.4 copy.33
  458.3 60.8 %convolution_bitcast_fusion = f32[16,256,2048]{1,2,0:T(8,128)} fusion(f32[2,16,1,256,256]{4,3,1,2,0:T(8,128)} %bitcast.100, f32[256,2048]{1,0:T(8,128)} %reduce_sum.37), kind=kOutput, calls=%fused_computation.6 | convolution fusion | flops 25769803776 | bytes 39845888 | tf_op jit(solution)/shard_map/rab,bc->rac/dot_general | solution.py:37
  519.1 18.1 %fusion.1 = f32[8,256,2048]{1,2,0:T(8,128)} fusion(f32[16,256,2048]{1,2,0:T(8,128)} %convolution_bitcast_fusion, f32[16,256,2048]{1,2,0:T(8,128)} %fusion, f32[256,2048]{0,1:T(8,128)S(1)} %copy-done.1, pred[8]{0:T(512)(128)(4,1)S(1)} %bitcast.108, pred[8]{0:T(512)(128)(4,1)S(1)} %bitcast.107), kind=kLoop, calls=%fused_computation.9 | loop fusion | flops 12582912 | bytes 52428816 | tf_op jit(solution)/shard_map/jit(_where)/select_n | solution.py:42
  537.2 16.7 %copy.34 = f32[8,1,256,1,4,512]{5,2,0,3,1,4:T(8,128)} copy(f32[8,1,256,1,4,512]{2,5,4,0,3,1:T(8,128)} %bitcast.91) | data formatting | bytes 33554432 | tf_op jit(solution)/shard_map/reshape | solution.py:58
  553.9 367.8 %all_to_all.18 = f32[8,1,256,1,4,512]{5,2,0,3,1,4:T(8,128)S(1)} all-to-all(f32[8,1,256,1,4,512]{5,2,0,3,1,4:T(8,128)} %copy.34), channel_id=1, replica_groups=mesh['row'=4,'col'=8] {'row'}, dimensions={4} | all-to-all | bytes 33554432 | tf_op jit(solution)/shard_map/all_to_all | solution.py:59
  921.6 20.2 %copy.36 = f32[8,4,256,1,1,512]{5,4,3,2,1,0:T(1,128)} copy(f32[8,4,256,1,1,512]{5,2,0,1,4,3:T(8,128)S(1)} %bitcast.92) | data formatting | bytes 33554432
  941.9 14.3 %reduce_sum.38 = f32[512,8,256]{2,1,0:T(8,128)} reduce(f32[8,512,8,256]{3,2,1,0:T(8,128)} %all-gather.7.cloned.1.call-done, f32[]{:T(128)} %constant.27.clone.1), dimensions={0}, to_apply=%region_2.4 | reduce | flops 7340032 | bytes 37748740 | tf_op jit(solution)/shard_map/reduce_sum | solution.py:13
  956.1 14.4 %reduce_sum.39 = f32[512,8,256]{2,1,0:T(8,128)} reduce(f32[8,512,8,256]{3,2,1,0:T(8,128)} %all-gather.9.cloned.1.call-done, f32[]{:T(128)} %constant.27.clone.1), dimensions={0}, to_apply=%region_3.5 | reduce | flops 7340032 | bytes 37748740 | tf_op jit(solution)/shard_map/reduce_sum | solution.py:13
  970.5 7.4 pad_maximum_fusion
  977.9 9.9 copy.30
  987.8 59.2 %convolution_multiply_fusion = f32[4096,2048]{1,0:T(8,128)} fusion(f32[512,4096]{0,1:T(8,128)} %bitcast.105, f32[256,2048]{1,0:T(8,128)} %reduce_sum.37, f32[256,2048]{1,0:T(8,128)S(1)} %copy-done), kind=kOutput, calls=%fused_computation.7 | convolution fusion | flops 51549044736 | bytes 46137344 | tf_op jit(solution)/shard_map/dot_general | solution.py:53
  1047.0 48.3 %reshape.105 = f32[16,1,256,8,1,256]{5,4,3,2,1,0:T(1,128)} reshape(f32[4096,2048]{1,0:T(8,128)} %convolution_multiply_fusion) | data formatting | bytes 67108864 | tf_op jit(solution)/shard_map/reshape | solution.py:56
  (22 shorter events, 0.3 us)
Async XLA Ops:
  7.2 190.0 %all-gather.11.cloned.1.call-start = ((), (), s32[]{:S(2)}) async-start(), calls=%async_computation.3 | async-start | bytes 10485760 | tf_op jit(solution)/shard_map/all_gather | solution.py:13
  44.6 388.7 %all-gather.13.cloned.1.call-start = ((), (), s32[]{:S(2)}) async-start(), calls=%async_computation.4 | async-start | bytes 10485760 | tf_op jit(solution)/shard_map/all_gather | solution.py:13
  285.4 656.5 %all-gather.7.cloned.1.call-start = ((), (), s32[]{:S(2)}) async-start(), calls=%async_computation.1 | async-start | bytes 37748736 | tf_op jit(solution)/shard_map/all_gather | solution.py:13
  433.3 5.9 copy-start
  448.2 508.0 %all-gather.9.cloned.1.call-start = ((), (), s32[]{:S(2)}) async-start(), calls=%async_computation.2 | async-start | bytes 37748736 | tf_op jit(solution)/shard_map/all_gather | solution.py:13
  458.3 60.8 %copy-start.1 = (f32[256,2048]{0,1:T(8,128)S(1)}, f32[256,2048]{0,1:T(8,128)}, u32[]{:S(2)}) copy-start(f32[256,2048]{0,1:T(8,128)} %copy.33) | copy-start | bytes 6291460
Sparse Core Ops, SparseCore 0:
  44.8 152.3 all-gather.10
  285.5 147.7 all-gather.12
  448.3 158.8 all-gather.6
  608.9 160.6 all-gather.8
